TPU v7x, 128 devices: a whole 4x4x4 slice. The times are simulated.
128 devices in a mesh: slab: 4 (over y_lo, core), tile: 32 (over z, y_hi, x).
Axes of the slice: x: 4, y: 4 (y_hi: 2, y_lo: 2; y = y_hi * 2 + y_lo), z: 4, core: 2. Of those that a mesh axis runs over, the one named last changes fastest.
Arguments:
- electric: float32 [3, 56, 1024, 1024], P(None, 'slab', 'tile'), may hold values from -6 to 6
- current: float32 [3, 56, 1024, 1024], P(None, 'slab', 'tile'), may hold values from -6 to 6
- mass_shift: float32 [56, 1024, 1024], P('slab', 'tile'), may hold values from 0.5 to 4
- interface: float32 [4, 2, 2, 1024, 1024], P('slab', None, None, 'tile'), may hold values from -6 to 6
- auxiliary: float32 [4, 2, 4, 2, 1024, 1024], P('slab', None, None, None, 'tile'), may hold values from -3 to 3
Outputs:
- smoothed: float32 [3, 56, 1024, 1024], P(None, 'slab', 'tile')
- next_interface: float32 [4, 2, 2, 1024, 1024], P('slab', None, None, 'tile')
- next_auxiliary: float32 [4, 2, 4, 2, 1024, 1024], P('slab', None, None, None, 'tile')
All inputs are finite; a program needn't handle non-finite values.
Results may differ from a plain program's by a relative error of at most 0.0001.
Values sent between devices are 32-bit elements; how exact they have to be, the bound alone decides.
A program may use at most 128 MiB of HBM per device.

v0:
```python
import math

import jax
import jax.numpy as jnp
from jax import lax
from jax.sharding import PartitionSpec as P

pade_weights = [2.0 / 9.0 * math.sin(j * math.pi / 9.0) ** 2 for j in range(1, 5)]
pade_decays = [math.cos(j * math.pi / 9.0) ** 2 for j in range(1, 5)]


def extended(cells, sides, width):
    for axis, dim in sides:
        count = lax.axis_size(axis)
        ends = count - 1
        head = lax.slice_in_dim(cells, 0, width, axis=dim)
        tail = lax.slice_in_dim(cells, cells.shape[dim] - width, cells.shape[dim], axis=dim)
        cells = jnp.concatenate(
            [
                lax.ppermute(tail, axis, [(i, (i + 1) % count) for i in range(ends)]),
                cells,
                lax.ppermute(head, axis, [((i + 1) % count, i) for i in range(ends)]),
            ],
            axis=dim,
        )
    return cells


def from_behind(block, axis, distance):
    devices = range(lax.axis_size(axis))
    route = [(i - distance, i) for i in devices if i - distance in devices]
    return lax.ppermute(block, axis, route)


def forward_diff(values, along):
    along = along % values.ndim
    count = values.shape[along]
    shifted = jnp.concatenate(
        [
            lax.slice_in_dim(values, 1, count, axis=along),
            jnp.zeros_like(lax.slice_in_dim(values, 0, 1, axis=along)),
        ],
        along,
    )
    return shifted - values


def backward_diff(values, along):
    along = along % values.ndim
    count = values.shape[along]
    shifted = jnp.concatenate(
        [
            jnp.zeros_like(lax.slice_in_dim(values, 0, 1, axis=along)),
            lax.slice_in_dim(values, 0, count - 1, axis=along),
        ],
        along,
    )
    return values - shifted


def curl_curl(padded):
    field_x, field_y, field_z = (padded[0], padded[1], padded[2])
    flux_x = forward_diff(field_z, 1) - forward_diff(field_y, 0)
    flux_y = forward_diff(field_x, 0) - forward_diff(field_z, 2)
    flux_z = forward_diff(field_y, 2) - forward_diff(field_x, 1)
    image_x = backward_diff(flux_z, 1) - backward_diff(flux_y, 0)
    image_y = backward_diff(flux_x, 0) - backward_diff(flux_z, 2)
    image_z = backward_diff(flux_y, 2) - backward_diff(flux_x, 1)
    return jnp.stack([image_x, image_y, image_z])[:, 1:-1, 1:-1, :]


def update(padded, current, mass_shift):
    interior = padded[:, 1:-1, 1:-1, :]
    residual = current - (curl_curl(padded) + mass_shift * interior)
    return interior + 0.5 * residual / (mass_shift + 4.0)


def surface(padded):
    comp_x = padded[..., 0, :, :]
    comp_y = padded[..., 1, :, :]
    divergence = backward_diff(comp_x, -1) + backward_diff(comp_y, -2)
    rotation = forward_diff(comp_y, -1) - forward_diff(comp_x, -2)
    vort_x = backward_diff(rotation, -2) - forward_diff(divergence, -1)
    vort_y = -backward_diff(rotation, -1) - forward_diff(divergence, -2)
    return (jnp.stack([vort_x, vort_y], axis=-3) / 8.0)[..., 1:-1, :]


def shards(electric, current, mass_shift, interface, auxiliary):
    weights = jnp.asarray(pade_weights, jnp.float32).reshape(1, 4, 1, 1, 1)
    decays = jnp.asarray(pade_decays, jnp.float32).reshape(1, 4, 1, 1, 1)
    strip = electric.shape[2]
    width = electric.shape[3]
    zero_plane = jnp.zeros((1, strip, width), jnp.float32)
    below_ghost = jnp.concatenate([interface[0, 0], zero_plane], 0)
    above_ghost = jnp.concatenate([interface[0, 1], zero_plane], 0)
    local_field = electric
    for sweep_index in range(2):
        padded = extended(
            jnp.concatenate([below_ghost[:, None], local_field, above_ghost[:, None]], 1),
            (("tile", 2),),
            1,
        )
        local_field = update(padded, current, mass_shift)
    traces = jnp.stack([local_field[0:2, 0], local_field[0:2, -1]])
    combined = traces[:, None] - decays * auxiliary[0]
    padded_surface = extended(combined, (("tile", 3),), 1)
    new_auxiliary = surface(padded_surface)
    outgoing = traces + jnp.sum(weights * new_auxiliary, axis=1)
    from_below = from_behind(outgoing[1], "slab", 1)
    from_above = from_behind(outgoing[0], "slab", -1)
    next_interface = jnp.stack([from_below, from_above])[None]
    return (local_field, next_interface, new_auxiliary[None])


def solution(mesh):
    placed = (
        P(None, "slab", "tile", None),
        P(None, "slab", "tile", None),
        P("slab", "tile", None),
        P("slab", None, None, "tile", None),
        P("slab", None, None, None, "tile", None),
    )
    return jax.shard_map(
        shards,
        mesh=mesh,
        in_specs=placed,
        out_specs=(
            P(None, "slab", "tile", None),
            P("slab", None, None, "tile", None),
            P("slab", None, None, None, "tile", None),
        ),
        check_vma=False,
    )
```

profile of v0, /device:TPU:97, one launch (start us, length us, event | category | flops | bytes accessed | tf_op | source)
XLA Modules:
  0.0 142.7 jit_solution(16562079701576884013)
XLA Ops:
  1.8 3.6 %pad_maximum_fusion.5 = f32[3,16,32,1024]{3,2,1,0:T(8,128)S(1)} fusion(f32[3,1,32,1024]{3,2,1,0:T(8,128)S(1)} %get-tuple-element.45, f32[3,1,32,1024]{3,2,1,0:T(8,128)S(1)} %get-tuple-element.46, f32[3,14,32,1024]{3,2,1,0:T(8,128)} %param.7), kind=kLoop, calls=%fused_computation.5 | loop fusion | flops 3145728 | bytes 12582912 | tf_op jit(solution)/shard_map/concatenate | solution.py:99
  5.8 3.1 %collective-permute-start = (f32[3,16,1,1024]{3,2,1,0:T(1,128)S(1)}, f32[3,16,1,1024]{3,2,1,0:T(1,128)S(1)}, u32[]{:S(2)}, u32[]{:S(2)}) collective-permute-start(f32[3,16,1,1024]{3,2,1,0:T(1,128)S(1)} %get-tuple-element.21), channel_id=1, source_target_pairs={{0,1},{1,2},{2,3},{3,4},{4,5},{5,6},{6,7},{7,8},{8,9},{9,10},{10,1... | collective-permute-start | bytes 589832 | tf_op jit(solution)/shard_map/ppermute | solution.py:20
  8.9 6.7 %collective-permute-start.1 = (f32[3,16,1,1024]{3,2,1,0:T(1,128)S(1)}, f32[3,16,1,1024]{3,2,1,0:T(1,128)S(1)}, u32[]{:S(2)}, u32[]{:S(2)}) collective-permute-start(f32[3,16,1,1024]{3,2,1,0:T(1,128)S(1)} %get-tuple-element.22), channel_id=1, source_target_pairs={{1,0},{2,1},{3,2},{4,3},{5,4},{6,5},{7,6},{8,7},{9,8},{10,9},{11,1... | collective-permute-start | bytes 589832 | tf_op jit(solution)/shard_map/ppermute | solution.py:22
  15.8 2.1 %collective-permute-done = f32[3,16,1,1024]{3,2,1,0:T(1,128)S(1)} collective-permute-done((f32[3,16,1,1024]{3,2,1,0:T(1,128)S(1)}, f32[3,16,1,1024]{3,2,1,0:T(1,128)S(1)}, u32[]{:S(2)}, u32[]{:S(2)}) %collective-permute-start) | collective-permute-done | bytes 196640 | tf_op jit(solution)/shard_map/ppermute | solution.py:20
  18.9 1.9 %fusion.1 = f32[3,16,34,1024]{3,2,1,0:T(8,128)S(1)} fusion(f32[3,1,32,1024]{3,2,1,0:T(8,128)S(1)} %get-tuple-element.45, f32[3,1,32,1024]{3,2,1,0:T(8,128)S(1)} %get-tuple-element.46, f32[3,16,1,1024]{3,2,1,0:T(1,128)S(1)} %collective-permute-done.1, f32[3,14,32,1024]{3,2,1,0:T(8,128)S(1)} %bitcast.117, f32[3,16,1,1024]{3,2,1,0:T(1,128)S(1)} %collective-permute-done), kind=kLoop, calls=%fused_computation.9 | loop fusion | flops 6684672 | bytes 13369344 | tf_op jit(solution)/shard_map/concatenate | solution.py:18
  20.8 2.7 %slice_bitcast_fusion.9 = (f32[15,34,1024]{2,1,0:T(8,128)}, f32[15,34,1024]{2,1,0:T(8,128)}) fusion(f32[3,16,34,1024]{3,2,1,0:T(8,128)S(1)} %fusion.1), kind=kLoop, calls=%fused_computation.48 | loop fusion | bytes 8355840 | tf_op jit(solution)/shard_map/slice | solution.py:40
  25.0 1.9 %slice.251 = f32[16,33,1024]{2,1,0:T(8,128)} slice(f32[16,34,1024]{2,1,0:T(8,128)S(1)} %get-tuple-element.15), slice={[0:16], [1:34], [0:1024]} | slice | bytes 4325376 | tf_op jit(solution)/shard_map/slice | solution.py:40
  26.9 2.3 %slice.249 = f32[16,34,1023]{2,1,0:T(8,128)} slice(f32[16,34,1024]{2,1,0:T(8,128)S(1)} %get-tuple-element.15), slice={[0:16], [0:34], [1:1024]} | slice | bytes 4452096 | tf_op jit(solution)/shard_map/slice | solution.py:40
  29.1 2.2 %slice.243 = f32[16,34,1023]{2,1,0:T(8,128)} slice(f32[16,34,1024]{2,1,0:T(8,128)S(1)} %get-tuple-element.14), slice={[0:16], [0:34], [1:1024]} | slice | bytes 4452096 | tf_op jit(solution)/shard_map/slice | solution.py:40
  31.3 1.9 %slice.245 = f32[16,33,1024]{2,1,0:T(8,128)} slice(f32[16,34,1024]{2,1,0:T(8,128)S(1)} %get-tuple-element.16), slice={[0:16], [1:34], [0:1024]} | slice | bytes 4325376 | tf_op jit(solution)/shard_map/slice | solution.py:40
  33.2 6.9 %subtract_subtract_fusion.5 = (f32[16,34,1024]{2,1,0:T(8,128)S(1)}, f32[16,34,1024]{2,1,0:T(8,128)S(1)}, f32[16,34,1024]{2,1,0:T(8,128)S(1)}) fusion(f32[16,33,1024]{2,1,0:T(8,128)} %slice.245, f32[16,34,1023]{2,1,0:T(8,128)} %slice.243, f32[3,16,34,1024]{3,2,1,0:T(8,128)S(1)} %fusion.1, f32[16,34,1023]{2,1,0:T(8,128)} %slice.249, ...), kind=kLoop, calls=%fused_computation.44 | loop fusion | flops 5013504 | bytes 26324736 | tf_op jit(solution)/shard_map/sub | solution.py:65
  41.7 1.7 %slice.253 = f32[15,34,1024]{2,1,0:T(8,128)} slice(f32[16,34,1024]{2,1,0:T(8,128)S(1)} %get-tuple-element.13), slice={[0:15], [0:34], [0:1024]} | slice | bytes 4177920 | tf_op jit(solution)/shard_map/slice | solution.py:54
  43.4 7.3 %subtract_bitcast_fusion.5 = (f32[1,16,34,1024]{3,2,1,0:T(8,128)}, f32[1,16,34,1024]{3,2,1,0:T(8,128)}, f32[1,16,34,1024]{3,2,1,0:T(8,128)}) fusion(f32[16,34,1024]{2,1,0:T(8,128)S(1)} %get-tuple-element.12, f32[15,34,1024]{2,1,0:T(8,128)} %slice.250, f32[16,34,1024]{2,1,0:T(8,128)S(1)} %get-tuple-element.11, f32[16,33,1024]{2,1,0:T(8,128)S(1)} %bitcast.118, ...), kind=kLoop, calls=%fused_computation.42 | loop fusion | flops 5013504 | bytes 26324736 | tf_op jit(solution)/shard_map/stack | solution.py:69
  50.8 4.8 %fusion.13 = f32[3,14,32,1024]{3,2,1,0:T(8,128)S(1)} fusion(f32[3,14,32,1024]{3,2,1,0:T(8,128)S(1)} %bitcast.117, f32[3,14,32,1024]{3,2,1,0:T(8,128)S(1)} %bitcast.127, f32[1,16,34,1024]{3,2,1,0:T(8,128)} %get-tuple-element.38, f32[1,16,34,1024]{3,2,1,0:T(8,128)} %get-tuple-element.37, f32[1,16,34,1024]{3,2,1,0:T(8,128)} %get-tuple-element.36, ...), kind=kLoop, calls=%fused_computation.24 | loop fusion | flops 11010048 | bytes 26869760 | tf_op jit(solution)/shard_map/add | solution.py:75
  57.0 1.9 %collective-permute-start.2 = (f32[3,16,1,1024]{3,2,1,0:T(1,128)S(1)}, f32[3,16,1,1024]{3,2,1,0:T(1,128)S(1)}, u32[]{:S(2)}, u32[]{:S(2)}) collective-permute-start(f32[3,16,1,1024]{3,2,1,0:T(1,128)S(1)} %get-tuple-element.19), channel_id=1, source_target_pairs={{0,1},{1,2},{2,3},{3,4},{4,5},{5,6},{6,7},{7,8},{8,9},{9,10},{10,1... | collective-permute-start | bytes 589832 | tf_op jit(solution)/shard_map/ppermute | solution.py:20
  59.0 8.8 %collective-permute-start.3 = (f32[3,16,1,1024]{3,2,1,0:T(1,128)S(1)}, f32[3,16,1,1024]{3,2,1,0:T(1,128)S(1)}, u32[]{:S(2)}, u32[]{:S(2)}) collective-permute-start(f32[3,16,1,1024]{3,2,1,0:T(1,128)S(1)} %get-tuple-element.20), channel_id=1, source_target_pairs={{1,0},{2,1},{3,2},{4,3},{5,4},{6,5},{7,6},{8,7},{9,8},{10,9},{11,1... | collective-permute-start | bytes 589832 | tf_op jit(solution)/shard_map/ppermute | solution.py:22
  70.2 1.8 %fusion.3 = f32[3,16,34,1024]{3,2,1,0:T(8,128)S(1)} fusion(f32[3,1,32,1024]{3,2,1,0:T(8,128)S(1)} %get-tuple-element.45, f32[3,1,32,1024]{3,2,1,0:T(8,128)S(1)} %copy-done.2, f32[3,16,1,1024]{3,2,1,0:T(1,128)S(1)} %collective-permute-done.3, f32[3,14,32,1024]{3,2,1,0:T(8,128)S(1)} %fusion.13, f32[3,16,1,1024]{3,2,1,0:T(1,128)S(1)} %collective-permute-done.2), kind=kLoop, calls=%fused_computation.11 | loop fusion | flops 6684672 | bytes 13369344 | tf_op jit(solution)/shard_map/concatenate | solution.py:18
  72.1 2.7 %slice_bitcast_fusion.7 = (f32[15,34,1024]{2,1,0:T(8,128)}, f32[15,34,1024]{2,1,0:T(8,128)}) fusion(f32[3,16,34,1024]{3,2,1,0:T(8,128)S(1)} %fusion.3), kind=kLoop, calls=%fused_computation.46 | loop fusion | bytes 8355840 | tf_op jit(solution)/shard_map/slice | solution.py:40
  76.3 1.9 %slice.268 = f32[16,33,1024]{2,1,0:T(8,128)} slice(f32[16,34,1024]{2,1,0:T(8,128)S(1)} %get-tuple-element.7), slice={[0:16], [1:34], [0:1024]} | slice | bytes 4325376 | tf_op jit(solution)/shard_map/slice | solution.py:40
  78.1 2.3 %slice.266 = f32[16,34,1023]{2,1,0:T(8,128)} slice(f32[16,34,1024]{2,1,0:T(8,128)S(1)} %get-tuple-element.7), slice={[0:16], [0:34], [1:1024]} | slice | bytes 4452096 | tf_op jit(solution)/shard_map/slice | solution.py:40
  80.4 2.2 %slice.260 = f32[16,34,1023]{2,1,0:T(8,128)} slice(f32[16,34,1024]{2,1,0:T(8,128)S(1)} %get-tuple-element.6), slice={[0:16], [0:34], [1:1024]} | slice | bytes 4452096 | tf_op jit(solution)/shard_map/slice | solution.py:40
  82.6 1.9 %slice.262 = f32[16,33,1024]{2,1,0:T(8,128)} slice(f32[16,34,1024]{2,1,0:T(8,128)S(1)} %get-tuple-element.8), slice={[0:16], [1:34], [0:1024]} | slice | bytes 4325376 | tf_op jit(solution)/shard_map/slice | solution.py:40
  84.5 6.9 %subtract_subtract_fusion.2 = (f32[16,34,1024]{2,1,0:T(8,128)S(1)}, f32[16,34,1024]{2,1,0:T(8,128)S(1)}, f32[16,34,1024]{2,1,0:T(8,128)S(1)}) fusion(f32[16,33,1024]{2,1,0:T(8,128)} %slice.262, f32[16,34,1023]{2,1,0:T(8,128)} %slice.260, f32[3,16,34,1024]{3,2,1,0:T(8,128)S(1)} %fusion.3, f32[16,34,1023]{2,1,0:T(8,128)} %slice.266, ...), kind=kLoop, calls=%fused_computation.38 | loop fusion | flops 5013504 | bytes 26324736 | tf_op jit(solution)/shard_map/sub | solution.py:65
  94.7 7.3 %subtract_bitcast_fusion.2 = (f32[1,16,34,1024]{3,2,1,0:T(8,128)}, f32[1,16,34,1024]{3,2,1,0:T(8,128)}, f32[1,16,34,1024]{3,2,1,0:T(8,128)}) fusion(f32[16,34,1024]{2,1,0:T(8,128)S(1)} %get-tuple-element.4, f32[15,34,1024]{2,1,0:T(8,128)} %slice.267, f32[16,34,1024]{2,1,0:T(8,128)S(1)} %get-tuple-element.3, f32[16,33,1024]{2,1,0:T(8,128)S(1)} %bitcast.120, ...), kind=kLoop, calls=%fused_computation.36 | loop fusion | flops 5013504 | bytes 26324736 | tf_op jit(solution)/shard_map/stack | solution.py:69
  102.1 4.9 %fusion.8 = f32[3,14,32,1024]{3,2,1,0:T(8,128)S(1)} fusion(f32[3,14,32,1024]{3,2,1,0:T(8,128)S(1)} %fusion.13, f32[3,14,32,1024]{3,2,1,0:T(8,128)S(1)} %bitcast.129, f32[1,16,34,1024]{3,2,1,0:T(8,128)} %get-tuple-element.35, f32[1,16,34,1024]{3,2,1,0:T(8,128)} %get-tuple-element.34, f32[1,16,34,1024]{3,2,1,0:T(8,128)} %get-tuple-element.33, ...), kind=kLoop, calls=%fused_computation.17 | loop fusion | flops 11010048 | bytes 26869760 | tf_op jit(solution)/shard_map/add | solution.py:75
  107.4 2.0 %copy-done.3 = f32[3,14,32,1024]{3,2,1,0:T(8,128)} copy-done((f32[3,14,32,1024]{3,2,1,0:T(8,128)}, f32[3,14,32,1024]{3,2,1,0:T(8,128)S(1)}, u32[]{:S(2)}) %copy-start.3) | copy-done | bytes 5505048
  109.5 1.9 %collective-permute-start.4 = (f32[2,4,2,1,1024]{4,3,1,0,2:T(1,128)S(1)}, f32[2,4,2,1,1024]{4,3,1,0,2:T(1,128)S(1)}, u32[]{:S(2)}, u32[]{:S(2)}) collective-permute-start(f32[2,4,2,1,1024]{4,3,1,0,2:T(1,128)S(1)} %get-tuple-element.39), channel_id=1, source_target_pairs={{0,1},{1,2},{2,3},{3,4},{4,5},{5,6},{6,7},{7,8},{8,9},{9,10},{10,1... | collective-permute-start | bytes 196616 | tf_op jit(solution)/shard_map/ppermute | solution.py:20
  111.4 8.5 %collective-permute-start.5 = (f32[2,4,2,1,1024]{4,3,1,0,2:T(1,128)S(1)}, f32[2,4,2,1,1024]{4,3,1,0,2:T(1,128)S(1)}, u32[]{:S(2)}, u32[]{:S(2)}) collective-permute-start(f32[2,4,2,1,1024]{4,3,1,0,2:T(1,128)S(1)} %get-tuple-element.40), channel_id=1, source_target_pairs={{1,0},{2,1},{3,2},{4,3},{5,4},{6,5},{7,6},{8,7},{9,8},{10,9},{11,1... | collective-permute-start | bytes 196616 | tf_op jit(solution)/shard_map/ppermute | solution.py:22
  125.4 1.8 %fusion.16 = (f32[1,2,4,2,32,1024]{5,4,3,2,1,0:T(8,128)}, f32[2,2,32,1024]{3,2,1,0:T(8,128)S(1)}) fusion(f32[2,4,1,34,1024]{4,3,2,1,0:T(8,128)S(1)} %get-tuple-element.28, f32[2,4,1,34,1024]{4,3,2,1,0:T(8,128)S(1)} %get-tuple-element.27, f32[4]{0:T(128)S(1)} %copy-done.6), kind=kLoop, calls=%fused_computation.54 | loop fusion | flops 1966080 | bytes 4849680 | tf_op jit(solution)/shard_map/broadcast_in_dim | solution.py:112
  127.3 6.9 %collective-permute-start.6 = (f32[2,32,1024]{2,1,0:T(8,128)S(1)}, f32[2,32,1024]{2,1,0:T(8,128)S(1)}, u32[]{:S(2)}, u32[]{:S(2)}) collective-permute-start(f32[2,32,1024]{2,1,0:T(8,128)S(1)} %get-tuple-element.41), channel_id=1, source_target_pairs={{0,32},{32,64},{64,96},{1,33},{33,65},{65,97},{2,34},{34,66},{66,9... | collective-permute-start | bytes 786440 | tf_op jit(solution)/shard_map/ppermute | solution.py:32
  134.2 1.9 %collective-permute-start.7 = (f32[2,32,1024]{2,1,0:T(8,128)S(1)}, f32[2,32,1024]{2,1,0:T(8,128)S(1)}, u32[]{:S(2)}, u32[]{:S(2)}) collective-permute-start(f32[2,32,1024]{2,1,0:T(8,128)S(1)} %get-tuple-element.42), channel_id=1, source_target_pairs={{32,0},{64,32},{96,64},{33,1},{65,33},{97,65},{34,2},{66,34},{98,6... | collective-permute-start | bytes 786440 | tf_op jit(solution)/shard_map/ppermute | solution.py:32
  137.5 4.4 %collective-permute-done.7 = f32[2,32,1024]{2,1,0:T(8,128)S(1)} collective-permute-done((f32[2,32,1024]{2,1,0:T(8,128)S(1)}, f32[2,32,1024]{2,1,0:T(8,128)S(1)}, u32[]{:S(2)}, u32[]{:S(2)}) %collective-permute-start.7) | collective-permute-done | bytes 262176 | tf_op jit(solution)/shard_map/ppermute | solution.py:32
  (59 shorter events, 22.7 us)
Async XLA Ops:
  1.8 17.1 %copy-start.1 = (f32[3,1,32,1024]{3,2,1,0:T(8,128)}, f32[3,1,32,1024]{3,2,1,0:T(8,128)S(1)}, u32[]{:S(2)}) copy-start(f32[3,1,32,1024]{3,2,1,0:T(8,128)S(1)} %get-tuple-element.46) | copy-start | bytes 1179652
  1.8 17.1 %slice-start = ((s8[5505024]{0:T(1024)(128)(4,1)}), s8[4194304]{0:T(1024)(128)(4,1)S(1)}, s32[]{:S(2)}) async-start(s8[5505024]{0:T(1024)(128)(4,1)} %bitcast.116), calls=%async_computation | async-start | bytes 8388608
  1.8 13.8 %copy-start = (f32[14,32,1024]{2,1,0:T(8,128)S(1)}, f32[14,32,1024]{2,1,0:T(8,128)}, u32[]{:S(2)}) copy-start(f32[14,32,1024]{2,1,0:T(8,128)} %param.9) | copy-start | bytes 5505028
  1.8 17.1 %slice-start.1 = ((s8[5505024]{0:T(1024)(128)(4,1)}), s8[1310720]{0:T(1024)(128)(4,1)S(1)}, s32[]{:S(2)}) async-start(s8[5505024]{0:T(1024)(128)(4,1)} %bitcast.116), calls=%async_computation.1 | async-start | bytes 2621440
  5.8 12.2 %collective-permute-start = (f32[3,16,1,1024]{3,2,1,0:T(1,128)S(1)}, f32[3,16,1,1024]{3,2,1,0:T(1,128)S(1)}, u32[]{:S(2)}, u32[]{:S(2)}) collective-permute-start(f32[3,16,1,1024]{3,2,1,0:T(1,128)S(1)} %get-tuple-element.21), channel_id=1, source_target_pairs={{0,1},{1,2},{2,3},{3,4},{4,5},{5,6},{6,7},{7,8},{8,9},{9,10},{10,1... | collective-permute-start | bytes 589832 | tf_op jit(solution)/shard_map/ppermute | solution.py:20
  8.9 10.0 %collective-permute-start.1 = (f32[3,16,1,1024]{3,2,1,0:T(1,128)S(1)}, f32[3,16,1,1024]{3,2,1,0:T(1,128)S(1)}, u32[]{:S(2)}, u32[]{:S(2)}) collective-permute-start(f32[3,16,1,1024]{3,2,1,0:T(1,128)S(1)} %get-tuple-element.22), channel_id=1, source_target_pairs={{1,0},{2,1},{3,2},{4,3},{5,4},{6,5},{7,6},{8,7},{9,8},{10,9},{11,1... | collective-permute-start | bytes 589832 | tf_op jit(solution)/shard_map/ppermute | solution.py:22
  43.4 7.4 %slice-start.2 = ((s8[5505024]{0:T(1024)(128)(4,1)}), s8[4194304]{0:T(1024)(128)(4,1)S(1)}, s32[]{:S(2)}) async-start(s8[5505024]{0:T(1024)(128)(4,1)} %bitcast.126), calls=%async_computation.2 | async-start | bytes 8388608
  43.4 7.4 %slice-start.3 = ((s8[5505024]{0:T(1024)(128)(4,1)}), s8[1310720]{0:T(1024)(128)(4,1)S(1)}, s32[]{:S(2)}) async-start(s8[5505024]{0:T(1024)(128)(4,1)} %bitcast.126), calls=%async_computation.3 | async-start | bytes 2621440
  50.8 4.8 %copy-start.2 = (f32[3,1,32,1024]{3,2,1,0:T(8,128)S(1)}, f32[3,1,32,1024]{3,2,1,0:T(8,128)}, u32[]{:S(2)}) copy-start(f32[3,1,32,1024]{3,2,1,0:T(8,128)} %copy-done.1) | copy-start | bytes 1179652
  57.0 12.1 %collective-permute-start.2 = (f32[3,16,1,1024]{3,2,1,0:T(1,128)S(1)}, f32[3,16,1,1024]{3,2,1,0:T(1,128)S(1)}, u32[]{:S(2)}, u32[]{:S(2)}) collective-permute-start(f32[3,16,1,1024]{3,2,1,0:T(1,128)S(1)} %get-tuple-element.19), channel_id=1, source_target_pairs={{0,1},{1,2},{2,3},{3,4},{4,5},{5,6},{6,7},{7,8},{8,9},{9,10},{10,1... | collective-permute-start | bytes 589832 | tf_op jit(solution)/shard_map/ppermute | solution.py:20
  59.0 11.2 %collective-permute-start.3 = (f32[3,16,1,1024]{3,2,1,0:T(1,128)S(1)}, f32[3,16,1,1024]{3,2,1,0:T(1,128)S(1)}, u32[]{:S(2)}, u32[]{:S(2)}) collective-permute-start(f32[3,16,1,1024]{3,2,1,0:T(1,128)S(1)} %get-tuple-element.20), channel_id=1, source_target_pairs={{1,0},{2,1},{3,2},{4,3},{5,4},{6,5},{7,6},{8,7},{9,8},{10,9},{11,1... | collective-permute-start | bytes 589832 | tf_op jit(solution)/shard_map/ppermute | solution.py:22
  94.7 7.4 %slice-start.4 = ((s8[5505024]{0:T(1024)(128)(4,1)}), s8[4194304]{0:T(1024)(128)(4,1)S(1)}, s32[]{:S(2)}) async-start(s8[5505024]{0:T(1024)(128)(4,1)} %bitcast.128), calls=%async_computation.4 | async-start | bytes 8388608
  94.7 7.4 %slice-start.5 = ((s8[5505024]{0:T(1024)(128)(4,1)}), s8[1310720]{0:T(1024)(128)(4,1)S(1)}, s32[]{:S(2)}) async-start(s8[5505024]{0:T(1024)(128)(4,1)} %bitcast.128), calls=%async_computation.5 | async-start | bytes 2621440
  102.1 4.9 %copy-start.4 = (f32[1,2,4,2,32,1024]{5,4,3,2,1,0:T(8,128)S(1)}, f32[1,2,4,2,32,1024]{5,4,3,2,1,0:T(8,128)}, u32[]{:S(2)}) copy-start(f32[1,2,4,2,32,1024]{5,4,3,2,1,0:T(8,128)} %param.11) | copy-start | bytes 6291460
  102.1 4.9 %copy-start.5 = (f32[4]{0:T(128)S(1)}, f32[4]{0:T(128)}, u32[]{:S(2)}) copy-start(f32[4]{0:T(128)} %constant.11.clone) | copy-start | bytes 52
  106.9 2.4 %copy-start.3 = (f32[3,14,32,1024]{3,2,1,0:T(8,128)}, f32[3,14,32,1024]{3,2,1,0:T(8,128)S(1)}, u32[]{:S(2)}) copy-start(f32[3,14,32,1024]{3,2,1,0:T(8,128)S(1)} %fusion.8) | copy-start | bytes 16515076
  109.5 10.5 %collective-permute-start.4 = (f32[2,4,2,1,1024]{4,3,1,0,2:T(1,128)S(1)}, f32[2,4,2,1,1024]{4,3,1,0,2:T(1,128)S(1)}, u32[]{:S(2)}, u32[]{:S(2)}) collective-permute-start(f32[2,4,2,1,1024]{4,3,1,0,2:T(1,128)S(1)} %get-tuple-element.39), channel_id=1, source_target_pairs={{0,1},{1,2},{2,3},{3,4},{4,5},{5,6},{6,7},{7,8},{8,9},{9,10},{10,1... | collective-permute-start | bytes 196616 | tf_op jit(solution)/shard_map/ppermute | solution.py:20
  111.4 9.6 %collective-permute-start.5 = (f32[2,4,2,1,1024]{4,3,1,0,2:T(1,128)S(1)}, f32[2,4,2,1,1024]{4,3,1,0,2:T(1,128)S(1)}, u32[]{:S(2)}, u32[]{:S(2)}) collective-permute-start(f32[2,4,2,1,1024]{4,3,1,0,2:T(1,128)S(1)} %get-tuple-element.40), channel_id=1, source_target_pairs={{1,0},{2,1},{3,2},{4,3},{5,4},{6,5},{7,6},{8,7},{9,8},{10,9},{11,1... | collective-permute-start | bytes 196616 | tf_op jit(solution)/shard_map/ppermute | solution.py:22
  124.2 1.2 copy-start.6
  127.3 10.2 %collective-permute-start.6 = (f32[2,32,1024]{2,1,0:T(8,128)S(1)}, f32[2,32,1024]{2,1,0:T(8,128)S(1)}, u32[]{:S(2)}, u32[]{:S(2)}) collective-permute-start(f32[2,32,1024]{2,1,0:T(8,128)S(1)} %get-tuple-element.41), channel_id=1, source_target_pairs={{0,32},{32,64},{64,96},{1,33},{33,65},{65,97},{2,34},{34,66},{66,9... | collective-permute-start | bytes 786440 | tf_op jit(solution)/shard_map/ppermute | solution.py:32
  134.2 7.7 %collective-permute-start.7 = (f32[2,32,1024]{2,1,0:T(8,128)S(1)}, f32[2,32,1024]{2,1,0:T(8,128)S(1)}, u32[]{:S(2)}, u32[]{:S(2)}) collective-permute-start(f32[2,32,1024]{2,1,0:T(8,128)S(1)} %get-tuple-element.42), channel_id=1, source_target_pairs={{32,0},{64,32},{96,64},{33,1},{65,33},{97,65},{34,2},{66,34},{98,6... | collective-permute-start | bytes 786440 | tf_op jit(solution)/shard_map/ppermute | solution.py:32
where the time goes:
time: 146 us; the launch traced here: 143 us
  other arithmetic  52.5 us (36%)
  starting transfers between devices  39.8 us (27%)
  local copies, waits for them, and re-layouts  37.1 us (25%)
  waiting for transfers between devices  12.3 us (8%)
    ppermute x3, starting transfers between devices, extended(): lax.ppermute(head, axis, [((i + 1) % count, i) for i in range(ends)])  24 us
    slice x14, local copies, waits for them, and re-layouts, forward_diff(): lax.slice_in_dim(values, 1, count, axis=along)  23 us
    another operation x2, other arithmetic, curl_curl(): return jnp.stack([image_x, image_y, image_z])[:, 1:-1, 1:-1, :]  14.7 us
    sub x2, other arithmetic, curl_curl(): flux_z = forward_diff(field_y, 2) - forward_diff(field_x, 1)  13.9 us
    add x3, other arithmetic, update(): return interior + 0.5 * residual / (mass_shift + 4.0)  9.85 us
    ppermute x2, starting transfers between devices, from_behind(): return lax.ppermute(block, axis, route)  8.82 us
    ppermute x3, starting transfers between devices, extended(): lax.ppermute(tail, axis, [(i, (i + 1) % count) for i in range(ends)])  6.96 us
    slice x4, local copies, waits for them, and re-layouts, backward_diff(): lax.slice_in_dim(values, 0, count - 1, axis=along)  6.58 us
  transfers between devices with their start and end apart: 8, of which 7 were waited for; matrix products, arithmetic and copies ran while one was open for 0% of the time, Pallas kernels for 0%

commit v1 on v0

v1 whole, which is shorter than its diff:
```python
import functools
import math

import jax
import jax.numpy as jnp
from jax import lax
from jax.experimental import pallas as pl
from jax.experimental.pallas import tpu as pltpu
from jax.sharding import PartitionSpec as P

MESH = pl.DeviceIdType.MESH
TERMS = 4
pade_weights = [2.0 / 9.0 * math.sin(j * math.pi / 9.0) ** 2 for j in range(1, 5)]
pade_decays = [math.cos(j * math.pi / 9.0) ** 2 for j in range(1, 5)]
LANES = 128
PAD = 8


def kernel(
    n_slab,
    n_tile,
    electric,
    current,
    mass,
    interface,
    auxiliary,
    smoothed,
    next_if,
    next_aux,
    e0,
    e1,
    cur,
    mg,
    ax,
    tr,
    osum,
    out,
    pu1,
    pd1,
    ru1,
    rd1,
    pua,
    pda,
    rua,
    rda,
    pu2,
    pd2,
    ru2,
    rd2,
    pu3,
    pd3,
    ru3,
    rd3,
    load_sem,
    send_sem,
    recv_sem,
):
    planes, rows, width = electric.shape[1:]
    cols = width // LANES
    tiles = rows // 8
    depth = planes + 2
    tall = rows + 2 * PAD
    pitch = cols * tall
    last = PAD + rows - 1
    slab = lax.axis_index("slab")
    tile = lax.axis_index("tile")
    has_up = tile < n_tile - 1
    has_dn = tile > 0
    slab_up = slab < n_slab - 1
    slab_dn = slab > 0
    up = {"tile": tile + 1}
    dn = {"tile": tile - 1}
    sup = {"slab": slab + 1}
    sdn = {"slab": slab - 1}

    def columns(ref, c):
        return ref.at[..., pl.ds(c * LANES, LANES)]

    body = pl.ds(PAD, rows)
    e_loads = [
        pltpu.make_async_copy(
            columns(electric, c), e0.at[:, pl.ds(1, planes), c, body, :], load_sem.at[0, c]
        )
        for c in range(cols)
    ]
    ghosts = []
    for i, buf in enumerate((e0, e1)):
        for side in range(2):
            for c in range(cols):
                ghosts.append(
                    pltpu.make_async_copy(
                        columns(interface, c).at[0, side],
                        buf.at[pl.ds(0, 2), side * (depth - 1), c, body, :],
                        load_sem.at[1 + 2 * i + side, c],
                    )
                )
    a_loads = [
        pltpu.make_async_copy(
            columns(auxiliary, c).at[0], ax.at[:, :, :, c, body, :], load_sem.at[5, c]
        )
        for c in range(cols)
    ]
    m_load = pltpu.make_async_copy(mass, mg, load_sem.at[6, 0])
    c_load = pltpu.make_async_copy(current, cur, load_sem.at[6, 1])
    for copy in (*e_loads, *ghosts, *a_loads, m_load, c_load):
        copy.start()

    barrier = pltpu.get_barrier_semaphore()
    for there, who in ((has_up, up), (has_dn, dn), (slab_up, sup), (slab_dn, sdn)):

        @pl.when(there)
        def _():
            pl.semaphore_signal(barrier, inc=1, device_id=who, device_id_type=MESH)

    def exchange(slot, src_up, dst_up, src_dn, dst_dn):
        goes_up = pltpu.make_async_remote_copy(
            src_ref=src_up,
            dst_ref=dst_up,
            send_sem=send_sem.at[slot, 0],
            recv_sem=recv_sem.at[slot, 0],
            device_id=up,
            device_id_type=MESH,
        )
        goes_dn = pltpu.make_async_remote_copy(
            src_ref=src_dn,
            dst_ref=dst_dn,
            send_sem=send_sem.at[slot, 1],
            recv_sem=recv_sem.at[slot, 1],
            device_id=dn,
            device_id_type=MESH,
        )
        return goes_up, goes_dn

    def start(pair):
        @pl.when(has_up)
        def _():
            pair[0].start()

        @pl.when(has_dn)
        def _():
            pair[1].start()

    def arrived(pair):
        @pl.when(has_dn)
        def _():
            pair[0].wait_recv()

        @pl.when(has_up)
        def _():
            pair[1].wait_recv()

    def sent(pair):
        @pl.when(has_up)
        def _():
            pair[0].wait_send()

        @pl.when(has_dn)
        def _():
            pair[1].wait_send()

    first = exchange(0, pu1, ru1, pd1, rd1)
    aux_rows = exchange(1, pua, rua, pda, rda)
    second = exchange(2, pu2, ru2, pd2, rd2)
    third = exchange(3, pu3, ru3, pd3, rd3)
    slab_goes_up = pltpu.make_async_remote_copy(
        src_ref=out.at[1],
        dst_ref=next_if.at[0, 0],
        send_sem=send_sem.at[4, 0],
        recv_sem=recv_sem.at[4, 0],
        device_id=sup,
        device_id_type=MESH,
    )
    slab_goes_dn = pltpu.make_async_remote_copy(
        src_ref=out.at[0],
        dst_ref=next_if.at[0, 1],
        send_sem=send_sem.at[4, 1],
        recv_sem=recv_sem.at[4, 1],
        device_id=sdn,
        device_id_type=MESH,
    )

    flat0 = e0.reshape(3 * depth * pitch, LANES)
    flat1 = e1.reshape(3 * depth * pitch, LANES)
    flata = ax.reshape(2 * TERMS * 2 * pitch, LANES)
    flatt = tr.reshape(4 * pitch, LANES)
    zero_row = jnp.zeros((cols, LANES), jnp.float32)
    zero_tile = jnp.zeros((8, LANES), jnp.float32)

    def line(plane, row):
        return pl.ds(plane * pitch + row, cols, stride=tall)

    for buf in (e0, e1):
        for c in range(cols):
            for r in range(tall // 8):
                buf[2, 0, c, pl.ds(8 * r, 8), :] = zero_tile

    @pl.when(jnp.logical_not(has_dn))
    def _():
        for comp in range(3):

            @pl.loop(1, depth)
            def _(p):
                flat0[line(comp * depth + p, PAD - 1), :] = zero_row
                flat1[line(comp * depth + p, PAD - 1), :] = zero_row

        @pl.loop(0, 2 * TERMS * 2)
        def _(p):
            flata[line(p, PAD - 1), :] = zero_row

        for p in range(4):
            flatt[line(p, PAD - 1), :] = zero_row

    @pl.when(jnp.logical_not(has_up))
    def _():
        for comp in (0, 2):

            @pl.loop(1, depth)
            def _(p):
                flat0[line(comp * depth + p, last + 1), :] = zero_row
                flat1[line(comp * depth + p, last + 1), :] = zero_row

        @pl.loop(0, 2 * TERMS * 2)
        def _(p):
            flata[line(p, last + 1), :] = zero_row

        for p in range(4):
            flatt[line(p, last + 1), :] = zero_row

    @pl.when(jnp.logical_not(slab_dn))
    def _():
        next_if[0, 0] = jnp.zeros(next_if.shape[2:], jnp.float32)

    @pl.when(jnp.logical_not(slab_up))
    def _():
        next_if[0, 1] = jnp.zeros(next_if.shape[2:], jnp.float32)

    def pack(flat, to_up, to_dn):
        @pl.loop(0, planes)
        def _(k):
            for comp in range(3):
                to_up[comp * planes + k] = flat[line(comp * depth + 1 + k, last), :]
            for i, comp in enumerate((0, 2)):
                to_dn[i * planes + k] = flat[line(comp * depth + 1 + k, PAD), :]

    def unpack(flat, from_dn, from_up):
        @pl.when(has_dn)
        def _():
            @pl.loop(0, planes)
            def _(k):
                for comp in range(3):
                    flat[line(comp * depth + 1 + k, PAD - 1), :] = from_dn[comp * planes + k]

        @pl.when(has_up)
        def _():
            @pl.loop(0, planes)
            def _(k):
                for i, comp in enumerate((0, 2)):
                    flat[line(comp * depth + 1 + k, last + 1), :] = from_up[i * planes + k]

    lane = lax.broadcasted_iota(jnp.int32, (8, LANES), 1)
    not_last = lane < LANES - 1
    not_first = lane > 0

    def ahead(values):
        turned = [pltpu.roll(v, LANES - 1, 1) for v in values] + [zero_tile]
        return [jnp.where(not_last, turned[c], turned[c + 1]) for c in range(cols)]

    def behind(values):
        turned = [zero_tile] + [pltpu.roll(v, 1, 1) for v in values]
        return [jnp.where(not_first, turned[c + 1], turned[c]) for c in range(cols)]

    def sweep(src, k, r, first_sweep):
        top = PAD + 8 * r

        def take(comp, step_z, step_y):
            p = k + 1 + step_z
            return [src[comp, p, c, pl.ds(top + step_y, 8), :] for c in range(cols)]

        ex, ey, ez = take(0, 0, 0), take(1, 0, 0), take(2, 0, 0)
        exjp = take(0, 0, 1)
        eyr = ahead(ey)
        hz = [eyr[c] - ey[c] - exjp[c] + ex[c] for c in range(cols)]
        hzl = behind(hz)
        ezjp, eykp = take(2, 0, 1), take(1, 1, 0)
        ezkm, ezjpkm, eykm = take(2, -1, 0), take(2, -1, 1), take(1, -1, 0)
        hx = [(ezjp[c] - ez[c]) - (eykp[c] - ey[c]) for c in range(cols)]
        hxkm = [(ezjpkm[c] - ezkm[c]) - (ey[c] - eykm[c]) for c in range(cols)]
        image_y = [(hx[c] - hxkm[c]) - (hz[c] - hzl[c]) for c in range(cols)]
        eyjm = take(1, 0, -1)
        t = [(ey[c] - eyjm[c]) + (ez[c] - ezkm[c]) for c in range(cols)]
        tn = ahead(t)
        exjm, exkp, exkm = take(0, 0, -1), take(0, 1, 0), take(0, -1, 0)
        image_x = [
            (tn[c] - t[c]) + (4.0 * ex[c] - ((exjp[c] + exjm[c]) + (exkp[c] + exkm[c])))
            for c in range(cols)
        ]
        ezr = ahead(ez)
        hy = [(exkp[c] - ex[c]) - (ezr[c] - ez[c]) for c in range(cols)]
        hyl = behind(hy)
        ezjm, eyjmkp = take(2, 0, -1), take(1, 1, -1)
        hxjm = [(ez[c] - ezjm[c]) - (eyjmkp[c] - eyjm[c]) for c in range(cols)]
        image_z = [(hy[c] - hyl[c]) - (hx[c] - hxjm[c]) for c in range(cols)]
        news = []
        for c in range(cols):
            place = (k, pl.ds(8 * r, 8), pl.ds(c * LANES, LANES))
            if first_sweep:
                g = 0.5 / (mg[place] + 4.0)
                mg[place] = g
            else:
                g = mg[place]
            keep = 0.5 + 4.0 * g
            news.append(
                [
                    keep * old[c] + g * (cur[(comp, *place)] - image[c])
                    for comp, (old, image) in enumerate(
                        ((ex, image_x), (ey, image_y), (ez, image_z))
                    )
                ]
            )
        return news

    def first_sweep(which):
        @pl.loop(0, planes)
        def _(k):
            for r in which:
                news = sweep(e0, k, r, True)
                for c in range(cols):
                    for comp in range(3):
                        e1[comp, k + 1, c, pl.ds(PAD + 8 * r, 8), :] = news[c][comp]

    def second_sweep_inner(which):
        @pl.loop(1, planes - 1)
        def _(k):
            for r in which:
                news = sweep(e1, k, r, False)
                for c in range(cols):
                    for comp in range(3):
                        smoothed[
                            comp, k, pl.ds(8 * r, 8), pl.ds(c * LANES, LANES)
                        ] = news[c][comp]

    def second_sweep_ends(which):
        @pl.loop(0, 2)
        def _(side):
            k = side * (planes - 1)
            for r in which:
                news = sweep(e1, k, r, False)
                for c in range(cols):
                    for comp in range(3):
                        smoothed[
                            comp, k, pl.ds(8 * r, 8), pl.ds(c * LANES, LANES)
                        ] = news[c][comp]
                    for comp in range(2):
                        tr[side * 2 + comp, c, pl.ds(PAD + 8 * r, 8), :] = news[c][comp]

    edge_last = jnp.where(lane == LANES - 1, 3.0, 4.0)
    edge_first = jnp.where(lane == 0, 3.0, 4.0)

    def surface(read, comp, r):
        top = PAD + 8 * r
        u = [read(c, top) for c in range(cols)]
        ua, ub = ahead(u), behind(u)
        result = []
        for c in range(cols):
            if comp == 0 and c == cols - 1:
                centre = edge_last * u[c]
            elif comp == 1 and c == 0:
                centre = edge_first * u[c]
            else:
                centre = 4.0 * u[c]
            around = (ua[c] + ub[c]) + (read(c, top + 1) + read(c, top - 1))
            result.append(0.125 * (centre - around))
        return u, result

    def aux_surface(which):
        @pl.loop(0, 2)
        def _(side):
            for comp in range(2):
                for r in which:
                    total = [zero_tile] * cols
                    for j in range(TERMS):

                        def read(c, row):
                            return ax[side, j, comp, c, pl.ds(row, 8), :]

                        _, image = surface(read, comp, r)
                        for c in range(cols):
                            part = pade_decays[j] * image[c]
                            place = (pl.ds(8 * r, 8), pl.ds(c * LANES, LANES))
                            next_aux[(0, side, j, comp, *place)] = part
                            total[c] = total[c] + pade_weights[j] * part
                    for c in range(cols):
                        place = (pl.ds(8 * r, 8), pl.ds(c * LANES, LANES))
                        osum[(side, comp, *place)] = total[c]

    peers = sum(jnp.where(there, 1, 0) for there in (has_up, has_dn, slab_up, slab_dn))
    pl.semaphore_wait(barrier, peers)

    for copy in (*e_loads, *ghosts):
        copy.wait()
    pack(flat0, pu1, pd1)
    pu1[3 * planes] = flat0[line(depth + planes + 1, last), :]
    start(first)

    for copy in a_loads:
        copy.wait()

    @pl.loop(0, 2 * TERMS * 2)
    def _(p):
        pua[p] = flata[line(p, last), :]
        pda[p] = flata[line(p, PAD), :]

    start(aux_rows)
    m_load.wait()
    c_load.wait()
    inner = tuple(range(1, tiles - 1))
    outer = (0, tiles - 1)
    first_sweep(inner)
    arrived(first)
    unpack(flat0, ru1, rd1)

    @pl.when(has_dn)
    def _():
        row = ru1[3 * planes]
        flat0[line(depth + planes + 1, PAD - 1), :] = row
        flat1[line(depth + planes + 1, PAD - 1), :] = row

    first_sweep(outer)
    pack(flat1, pu2, pd2)
    start(second)

    aux_surface(inner)
    arrived(aux_rows)

    @pl.when(has_dn)
    def _():
        @pl.loop(0, 2 * TERMS * 2)
        def _(p):
            flata[line(p, PAD - 1), :] = rua[p]

    @pl.when(has_up)
    def _():
        @pl.loop(0, 2 * TERMS * 2)
        def _(p):
            flata[line(p, last + 1), :] = rda[p]

    aux_surface(outer)
    second_sweep_ends(inner)
    second_sweep_inner(inner)
    arrived(second)
    unpack(flat1, ru2, rd2)
    second_sweep_ends(outer)
    for p in range(4):
        pu3[p] = flatt[line(p, last), :]
        pd3[p] = flatt[line(p, PAD), :]
    start(third)
    second_sweep_inner(outer)
    arrived(third)

    @pl.when(has_dn)
    def _():
        for p in range(4):
            flatt[line(p, PAD - 1), :] = ru3[p]

    @pl.when(has_up)
    def _():
        for p in range(4):
            flatt[line(p, last + 1), :] = rd3[p]

    weight = sum(pade_weights)

    @pl.loop(0, 2)
    def _(side):
        for comp in range(2):
            for r in range(tiles):

                def read(c, row):
                    return tr[side * 2 + comp, c, pl.ds(row, 8), :]

                u, image = surface(read, comp, r)
                for c in range(cols):
                    place = (pl.ds(8 * r, 8), pl.ds(c * LANES, LANES))
                    out[(side, comp, *place)] = (
                        u[c] + weight * image[c] - osum[(side, comp, *place)]
                    )
                    osum[(side, comp, *place)] = image[c]

    @pl.when(slab_up)
    def _():
        slab_goes_up.start()

    @pl.when(slab_dn)
    def _():
        slab_goes_dn.start()

    @pl.loop(0, 2)
    def _(side):
        for comp in range(2):
            for r in range(tiles):
                for c in range(cols):
                    place = (pl.ds(8 * r, 8), pl.ds(c * LANES, LANES))
                    image = osum[(side, comp, *place)]
                    for j in range(TERMS):
                        where = (0, side, j, comp, *place)
                        next_aux[where] = image - next_aux[where]

    for pair in (first, aux_rows, second, third):
        sent(pair)

    @pl.when(slab_dn)
    def _():
        slab_goes_up.wait_recv()
        slab_goes_dn.wait_send()

    @pl.when(slab_up)
    def _():
        slab_goes_dn.wait_recv()
        slab_goes_up.wait_send()


def solution(mesh):
    n_slab, n_tile = mesh.shape["slab"], mesh.shape["tile"]

    def step(electric, current, mass_shift, interface, auxiliary):
        _, planes, rows, width = electric.shape
        cols = width // LANES
        tall = rows + 2 * PAD
        f32 = jnp.float32
        hbm = pl.BlockSpec(memory_space=pltpu.MemorySpace.HBM)
        vmem = pl.BlockSpec(memory_space=pltpu.VMEM)

        def lines(n):
            return pltpu.VMEM((n, cols, LANES), f32)

        return pl.pallas_call(
            functools.partial(kernel, n_slab, n_tile),
            out_shape=(
                pltpu.VMEM(electric.shape, f32),
                pltpu.VMEM(interface.shape, f32),
                pltpu.VMEM(auxiliary.shape, f32),
            ),
            in_specs=[hbm] * 5,
            out_specs=(vmem, vmem, vmem),
            scratch_shapes=[
                pltpu.VMEM((3, planes + 2, cols, tall, LANES), f32),
                pltpu.VMEM((3, planes + 2, cols, tall, LANES), f32),
                pltpu.VMEM(electric.shape, f32),
                pltpu.VMEM(mass_shift.shape, f32),
                pltpu.VMEM((2, TERMS, 2, cols, tall, LANES), f32),
                pltpu.VMEM((4, cols, tall, LANES), f32),
                pltpu.VMEM((2, 2, rows, width), f32),
                pltpu.VMEM((2, 2, rows, width), f32),
                lines(3 * planes + 1),
                lines(2 * planes),
                lines(3 * planes + 1),
                lines(2 * planes),
                lines(4 * TERMS),
                lines(4 * TERMS),
                lines(4 * TERMS),
                lines(4 * TERMS),
                lines(3 * planes),
                lines(2 * planes),
                lines(3 * planes),
                lines(2 * planes),
                lines(4),
                lines(4),
                lines(4),
                lines(4),
                pltpu.SemaphoreType.DMA((7, cols)),
                pltpu.SemaphoreType.DMA((5, 2)),
                pltpu.SemaphoreType.DMA((5, 2)),
            ],
            compiler_params=pltpu.CompilerParams(
                collective_id=0, has_side_effects=True, vmem_limit_bytes=44 * 2**20
            ),
        )(electric, current, mass_shift, interface, auxiliary)

    placed = (
        P(None, "slab", "tile", None),
        P(None, "slab", "tile", None),
        P("slab", "tile", None),
        P("slab", None, None, "tile", None),
        P("slab", None, None, None, "tile", None),
    )
    return jax.shard_map(
        step,
        mesh=mesh,
        in_specs=placed,
        out_specs=(
            P(None, "slab", "tile", None),
            P("slab", None, None, "tile", None),
            P("slab", None, None, None, "tile", None),
        ),
        check_vma=False,
    )
```

time: 146 us -> 40.6 us (0.28); the launches traced: 143 us -> 40.4 us
  other arithmetic: 52.5 us -> 0 us
  starting transfers between devices: 39.8 us -> 0 us
  Pallas kernels: 0 us -> 34.2 us
  local copies, waits for them, and re-layouts: 37.1 us -> 5.59 us
  waiting for transfers between devices: 12.3 us -> 0 us
    ppermute x8 -> x0, starting transfers between devices: 39.8 us -> none  [the longest x3 24 us: extended(): lax.ppermute(head, axis, [((i + 1) % count, i) for i in range(ends)])]
    pallas_call x0 -> x1, Pallas kernels: none -> 34.2 us  [step(): pl.pallas_call(functools.partial(kernel, n_slab, n_tile), out_shape=(pltp...]
    slice x21 -> x0, local copies, waits for them, and re-layouts: 30.4 us -> none  [the longest x14 23 us: forward_diff(): lax.slice_in_dim(values, 1, count, axis=along)]
    another operation x3 -> x0, other arithmetic: 15.8 us -> none  [the longest x2 14.7 us: curl_curl(): return jnp.stack([image_x, image_y, image_z])[:, 1:-1, 1:-1, :]]
    sub x4 -> x0, other arithmetic: 15.4 us -> none  [the longest x2 13.9 us: curl_curl(): flux_z = forward_diff(field_y, 2) - forward_diff(field_x, 1)]
    ppermute x8 -> x0, waiting for transfers between devices: 12.3 us -> none  [the longest x2 5.76 us: from_behind(): return lax.ppermute(block, axis, route)]
    add x4 -> x0, other arithmetic: 9.91 us -> none  [the longest x3 9.85 us: update(): return interior + 0.5 * residual / (mass_shift + 4.0)]
    concatenate x5 -> x0, other arithmetic: 8.78 us -> none  [the longest x2 4.64 us: shards(): jnp.concatenate([below_ghost[:, None], local_field, above_ghost[:, None]]...]
  transfers between devices with their start and end apart: 8 -> 0, of which waited for: 7 -> 0; matrix products, arithmetic and copies ran while one was open for 0% -> 0% of each run, Pallas kernels for 0% -> 0%
where the time goes in v1:
time: 40.6 us; the launch traced here: 40.4 us
  Pallas kernels  34.2 us (84%)
  local copies, waits for them, and re-layouts  5.59 us (14%)
  between operations  0.65 us (2%)
    pallas_call x1, Pallas kernels, step(): pl.pallas_call(functools.partial(kernel, n_slab, n_tile), out_shape=(pltp...  34.2 us
    unnamed x5, local copies, waits for them, and re-layouts  5.59 us

profile of v1, /device:TPU:97, one launch (start us, length us, event | category | flops | bytes accessed | tf_op | source)
XLA Modules:
  0.0 40.4 jit_solution(5047466921573363839)
XLA Ops:
  0.6 0.0 copy-start
  0.6 1.0 %copy-done = f32[1,2,2,32,1024]{4,3,2,1,0:T(8,128)S(1)} copy-done((f32[1,2,2,32,1024]{4,3,2,1,0:T(8,128)S(1)}, f32[1,2,2,32,1024]{4,3,2,1,0:T(8,128)}, u32[]{:S(2)}) %copy-start) | copy-done | bytes 524312
  1.7 34.2 %shard_map.76 = (f32[3,14,32,1024]{3,2,1,0:T(8,128)S(1)}, f32[1,2,2,32,1024]{4,3,2,1,0:T(8,128)S(1)}, f32[1,2,4,2,32,1024]{5,4,3,2,1,0:T(8,128)S(1)}) custom-call(f32[3,14,32,1024]{3,2,1,0:T(8,128)} %electric.1, f32[3,14,32,1024]{3,2,1,0:T(8,128)} %current.1, f32[14,32,1024]{2,1,0:T(8,128)} %mass.1, f32[1,2,2,32,1024]{4,3,2,1,0:T(8,128)S(1)} %copy-done, ...), custom_call_target="tpu_custom_call" | custom-call | tf_op jit(solution)/shard_map/pallas_call | solution.py:535
  35.9 2.4 %copy.11 = f32[3,14,32,1024]{3,2,1,0:T(8,128)} copy(f32[3,14,32,1024]{3,2,1,0:T(8,128)S(1)} %get-tuple-element.3) | data formatting | bytes 11010048
  38.3 0.8 %copy.12 = f32[1,2,2,32,1024]{4,3,2,1,0:T(8,128)} copy(f32[1,2,2,32,1024]{4,3,2,1,0:T(8,128)S(1)} %get-tuple-element.4) | data formatting | bytes 1048576
  39.1 1.3 %copy.13 = f32[1,2,4,2,32,1024]{5,4,3,2,1,0:T(8,128)} copy(f32[1,2,4,2,32,1024]{5,4,3,2,1,0:T(8,128)S(1)} %get-tuple-element.5) | data formatting | bytes 4194304
Async XLA Ops:
  0.6 1.0 %copy-start = (f32[1,2,2,32,1024]{4,3,2,1,0:T(8,128)S(1)}, f32[1,2,2,32,1024]{4,3,2,1,0:T(8,128)}, u32[]{:S(2)}) copy-start(f32[1,2,2,32,1024]{4,3,2,1,0:T(8,128)} %interface.1) | copy-start | bytes 1572868

commit v2 on v1

v2 whole, which is shorter than its diff:
```python
import functools
import math

import jax
import jax.numpy as jnp
from jax import lax
from jax.experimental import pallas as pl
from jax.experimental.pallas import tpu as pltpu
from jax.sharding import PartitionSpec as P

MESH = pl.DeviceIdType.MESH
TERMS = 4
pade_weights = [2.0 / 9.0 * math.sin(j * math.pi / 9.0) ** 2 for j in range(1, 5)]
pade_decays = [math.cos(j * math.pi / 9.0) ** 2 for j in range(1, 5)]
LANES = 128
PAD = 8
VMEM_LIMIT = 55 * 2**20 + 2**19


PAIRS = 2


def kernel(
    n_slab,
    n_tile,
    electric,
    current,
    mass,
    interface,
    auxiliary,
    smoothed,
    next_if,
    next_aux,
    e0,
    e1,
    cur,
    mg,
    ax,
    tr,
    osum,
    out,
    pu1,
    pd1,
    ru1,
    rd1,
    pua,
    pda,
    rua,
    rda,
    pu2,
    pd2,
    ru2,
    rd2,
    load_sem,
    send_sem,
    recv_sem,
):
    planes, rows, width = electric.shape[1:]
    cols = width // LANES
    tiles = rows // 8
    depth = planes + 2
    tall = rows + 2 * PAD
    pitch = cols * tall
    last = PAD + rows - 1
    inner = tuple(range(1, tiles - 1))
    outer = (0, tiles - 1)
    slab = lax.axis_index("slab")
    tile = lax.axis_index("tile")
    has_up = tile < n_tile - 1
    has_dn = tile > 0
    slab_up = slab < n_slab - 1
    slab_dn = slab > 0
    up = {"tile": tile + 1}
    dn = {"tile": tile - 1}
    sup = {"slab": slab + 1}
    sdn = {"slab": slab - 1}

    def columns(ref, c):
        return ref.at[..., pl.ds(c * LANES, LANES)]

    body = pl.ds(PAD, rows)

    def field_load(c, slot, row, count):
        return pltpu.make_async_copy(
            electric.at[:, :, pl.ds(row, count), pl.ds(c * LANES, LANES)],
            e0.at[:, pl.ds(1, planes), c, pl.ds(PAD + row, count), :],
            load_sem.at[slot, c],
        )

    edge_loads = [field_load(c, 0, 0, 8) for c in range(cols)]
    edge_loads += [field_load(c, 1, rows - 8, 8) for c in range(cols)]
    inner_loads = [field_load(c, 2, 8, rows - 16) for c in range(cols)]

    def ghost_loads(buf, slot):
        return [
            pltpu.make_async_copy(
                columns(interface, c).at[0, side],
                buf.at[pl.ds(0, 2), side * (depth - 1), c, body, :],
                load_sem.at[slot + side, c],
            )
            for side in range(2)
            for c in range(cols)
        ]

    ghosts0, ghosts1 = ghost_loads(e0, 3), ghost_loads(e1, 5)
    aux_loads = [
        pltpu.make_async_copy(
            columns(auxiliary, c).at[0], ax.at[:, :, :, c, body, :], load_sem.at[7, c]
        )
        for c in range(cols)
    ]
    m_load = pltpu.make_async_copy(mass, mg, load_sem.at[8, 0])
    c_load = pltpu.make_async_copy(current, cur, load_sem.at[8, 1])
    for copy in (*edge_loads, *ghosts0):
        copy.start()

    barrier = pltpu.get_barrier_semaphore()
    for there, who in ((has_up, up), (has_dn, dn), (slab_up, sup), (slab_dn, sdn)):

        @pl.when(there)
        def _():
            pl.semaphore_signal(barrier, inc=1, device_id=who, device_id_type=MESH)

    for copy in (*inner_loads, m_load, c_load, *ghosts1, *aux_loads):
        copy.start()

    def exchange(slot, src_up, dst_up, src_dn, dst_dn):
        goes_up = pltpu.make_async_remote_copy(
            src_ref=src_up,
            dst_ref=dst_up,
            send_sem=send_sem.at[slot, 0],
            recv_sem=recv_sem.at[slot, 0],
            device_id=up,
            device_id_type=MESH,
        )
        goes_dn = pltpu.make_async_remote_copy(
            src_ref=src_dn,
            dst_ref=dst_dn,
            send_sem=send_sem.at[slot, 1],
            recv_sem=recv_sem.at[slot, 1],
            device_id=dn,
            device_id_type=MESH,
        )
        return goes_up, goes_dn

    def part(slot, bufs, at, count):
        return exchange(slot, *(buf.at[pl.ds(at, count)] for buf in bufs))

    def start(pair):
        @pl.when(has_up)
        def _():
            pair[0].start()

        @pl.when(has_dn)
        def _():
            pair[1].start()

    def arrived(pair):
        @pl.when(has_dn)
        def _():
            pair[0].wait_recv()

        @pl.when(has_up)
        def _():
            pair[1].wait_recv()

    def sent(pair):
        @pl.when(has_up)
        def _():
            pair[0].wait_send()

        @pl.when(has_dn)
        def _():
            pair[1].wait_send()

    far = planes - 3
    near1 = ((0, 2, 0), (far, planes, 4))
    rest1 = ((2, far, 10),)
    near2 = ((0, 1, 0), (planes - 2, planes, 2))
    rest2 = ((1, planes - 2, 12),)
    first_near = part(0, (pu1, ru1, pd1, rd1), 0, 10)
    first_rest = part(1, (pu1, ru1, pd1, rd1), 10, 2 * (planes - 5))
    aux_rows = exchange(2, pua, rua, pda, rda)
    second_near = part(3, (pu2, ru2, pd2, rd2), 0, 12)
    second_rest = part(4, (pu2, ru2, pd2, rd2), 12, 2 * (planes - 3))
    slab_goes_up = pltpu.make_async_remote_copy(
        src_ref=out.at[1],
        dst_ref=next_if.at[0, 0],
        send_sem=send_sem.at[5, 0],
        recv_sem=recv_sem.at[5, 0],
        device_id=sup,
        device_id_type=MESH,
    )
    slab_goes_dn = pltpu.make_async_remote_copy(
        src_ref=out.at[0],
        dst_ref=next_if.at[0, 1],
        send_sem=send_sem.at[5, 1],
        recv_sem=recv_sem.at[5, 1],
        device_id=sdn,
        device_id_type=MESH,
    )

    flat0 = e0.reshape(3 * depth * pitch, LANES)
    flat1 = e1.reshape(3 * depth * pitch, LANES)
    flata = ax.reshape(2 * TERMS * 2 * pitch, LANES)
    flatt = tr.reshape(6 * pitch, LANES)
    zero_row = jnp.zeros((cols, LANES), jnp.float32)
    zero_tile = jnp.zeros((8, LANES), jnp.float32)

    def line(plane, row):
        return pl.ds(plane * pitch + row, cols, stride=tall)

    for buf in (e0, e1):
        for c in range(cols):
            for r in range(tall // 8):
                buf[2, 0, c, pl.ds(8 * r, 8), :] = zero_tile

    @pl.loop(1, depth)
    def _(p):
        for flat in (flat0, flat1):
            for comp in range(3):
                flat[line(comp * depth + p, PAD - 1), :] = zero_row
            for comp in (0, 2):
                flat[line(comp * depth + p, last + 1), :] = zero_row

    @pl.loop(0, 2 * TERMS * 2)
    def _(p):
        flata[line(p, PAD - 1), :] = zero_row
        flata[line(p, last + 1), :] = zero_row

    for p in range(4):
        flatt[line(p, PAD - 1), :] = zero_row
        flatt[line(p, last + 1), :] = zero_row

    @pl.when(jnp.logical_not(slab_dn))
    def _():
        next_if[0, 0] = jnp.zeros(next_if.shape[2:], jnp.float32)

    @pl.when(jnp.logical_not(slab_up))
    def _():
        next_if[0, 1] = jnp.zeros(next_if.shape[2:], jnp.float32)

    lane = lax.broadcasted_iota(jnp.int32, (8, LANES), 1)
    not_last = lane < LANES - 1
    not_first = lane > 0
    sub = lax.broadcasted_iota(jnp.int32, (cols, LANES), 0)
    row_lane = lax.broadcasted_iota(jnp.int32, (cols, LANES), 1)

    def row_ahead(row):
        turned = pltpu.roll(row, LANES - 1, 1)
        wrapped = jnp.where(sub < cols - 1, pltpu.roll(turned, cols - 1, 0), 0.0)
        return jnp.where(row_lane < LANES - 1, turned, wrapped)

    def row_behind(row):
        turned = pltpu.roll(row, 1, 1)
        wrapped = jnp.where(sub > 0, pltpu.roll(turned, 1, 0), 0.0)
        return jnp.where(row_lane > 0, turned, wrapped)

    def pack(flat, to_up, to_dn, spans):
        for low, high, at in spans:

            @pl.loop(low, high)
            def _(k):
                spot = at + PAIRS * (k - low)
                ey = flat[line(depth + 1 + k, last), :]
                over = flat[line(depth + 2 + k, last), :]
                to_up[spot] = (row_ahead(ey) - ey) + flat[line(1 + k, last), :]
                to_up[spot + 1] = flat[line(2 * depth + 1 + k, last), :] + (over - ey)
                to_dn[spot] = flat[line(1 + k, PAD), :]
                to_dn[spot + 1] = flat[line(2 * depth + 1 + k, PAD), :]

    def unpack(flat, from_dn, from_up, spans):
        for there, source, row in ((has_dn, from_dn, PAD - 1), (has_up, from_up, last + 1)):

            @pl.when(there)
            def _():
                for low, high, at in spans:

                    @pl.loop(low, high)
                    def _(k):
                        spot = at + PAIRS * (k - low)
                        flat[line(1 + k, row), :] = source[spot]
                        flat[line(2 * depth + 1 + k, row), :] = source[spot + 1]

    def back(value):
        return pltpu.roll(value, LANES - 1, 1)

    def forth(value):
        return pltpu.roll(value, 1, 1)

    def sweep(src, k, r, initial, write):
        top = PAD + 8 * r

        def at(comp, step_z, step_y, c):
            return src[comp, k + 1 + step_z, c, pl.ds(top + step_y, 8), :]

        def opening(c):
            if c == cols:
                return (None, None, None), (zero_tile,) * 3
            ey, ez = at(1, 0, 0, c), at(2, 0, 0, c)
            t = (ey - at(1, 0, -1, c)) + (ez - at(2, -1, 0, c))
            return (ey, ez, t), (back(ey), back(ez), back(t))

        here, turned = opening(0)
        hz_before = hy_before = zero_tile
        for c in range(cols):
            there, turned_there = opening(c + 1)
            ey, ez, t = here
            eyr, ezr, tn = (jnp.where(not_last, a, b) for a, b in zip(turned, turned_there))
            ex, exjp, exkp = at(0, 0, 0, c), at(0, 0, 1, c), at(0, 1, 0, c)
            hz = (eyr - ey) - (exjp - ex)
            hy = (exkp - ex) - (ezr - ez)
            hz_turned, hy_turned = forth(hz), forth(hy)
            dhz = hz - jnp.where(not_first, hz_turned, hz_before)
            dhy = hy - jnp.where(not_first, hy_turned, hy_before)
            place = (k, pl.ds(8 * r, 8), pl.ds(c * LANES, LANES))
            if initial:
                g = 0.5 / (mg[place] + 4.0)
                mg[place] = g
            else:
                g = mg[place]
            keep = 0.5 + 2.0 * g
            around = (exjp + at(0, 0, -1, c)) + (exkp + at(0, -1, 0, c))
            new_x = 0.5 * ex + g * ((cur[(0, *place)] + around) - (tn - t))
            eykp, ezjp = at(1, 1, 0, c), at(2, 0, 1, c)
            around = ((eykp + at(1, -1, 0, c)) - (ezjp - ez)) + (
                at(2, -1, 1, c) - at(2, -1, 0, c)
            )
            new_y = keep * ey + g * ((cur[(1, *place)] + around) + dhz)
            around = ((ezjp + at(2, 0, -1, c)) - (eykp - ey)) + (
                at(1, 1, -1, c) - at(1, 0, -1, c)
            )
            new_z = keep * ez + g * ((cur[(2, *place)] + around) - dhy)
            write(c, (new_x, new_y, new_z), g)
            here, turned = there, turned_there
            hz_before, hy_before = hz_turned, hy_turned

    def first_sweep(which, low, high, gap=0):
        @pl.loop(low, high)
        def _(step):
            k = step + (step // 2) * gap if gap else step
            for r in which:

                def write(c, news, g):
                    for comp in range(3):
                        e1[comp, k + 1, c, pl.ds(PAD + 8 * r, 8), :] = news[comp]

                sweep(e0, k, r, True, write)

    def second_sweep_inner(which):
        @pl.loop(1, planes - 1)
        def _(k):
            for r in which:

                def write(c, news, g):
                    place = (k, pl.ds(8 * r, 8), pl.ds(c * LANES, LANES))
                    for comp in range(3):
                        smoothed[(comp, *place)] = news[comp]

                sweep(e1, k, r, False, write)

    def second_sweep_ends(which):
        @pl.loop(0, 2)
        def _(side):
            k = side * (planes - 1)
            for r in which:

                def write(c, news, g):
                    place = (k, pl.ds(8 * r, 8), pl.ds(c * LANES, LANES))
                    for comp in range(3):
                        smoothed[(comp, *place)] = news[comp]
                    for comp in range(2):
                        tr[side * 2 + comp, c, pl.ds(PAD + 8 * r, 8), :] = news[comp]
                    tr[4 + side, c, pl.ds(PAD + 8 * r, 8), :] = g

                sweep(e1, k, r, False, write)

    edge_last = jnp.where(lane == LANES - 1, 3.0, 4.0)
    edge_first = jnp.where(lane == 0, 3.0, 4.0)

    def surface(read, comp, r, scale, write):
        top = PAD + 8 * r
        u = read(0, top)
        turned, before = back(u), zero_tile
        for c in range(cols):
            if c + 1 < cols:
                u_there = read(c + 1, top)
                turned_there = back(u_there)
            else:
                u_there, turned_there = None, zero_tile
            after = jnp.where(not_last, turned, turned_there)
            fore = forth(u)
            behind = jnp.where(not_first, fore, before)
            if comp == 0 and c == cols - 1:
                centre = (edge_last * (scale / 8)) * u
            elif comp == 1 and c == 0:
                centre = (edge_first * (scale / 8)) * u
            else:
                centre = (scale / 2) * u
            around = (after + behind) + (read(c, top + 1) + read(c, top - 1))
            write(c, u, centre - (scale / 8) * around)
            u, turned, before = u_there, turned_there, fore

    def aux_surface(which):
        @pl.loop(0, 2)
        def _(side):
            for comp in range(2):
                for r in which:
                    for j in range(TERMS):

                        def read(c, row):
                            return ax[side, j, comp, c, pl.ds(row, 8), :]

                        def write(c, u, image):
                            place = (pl.ds(8 * r, 8), pl.ds(c * LANES, LANES))
                            next_aux[(0, side, j, comp, *place)] = image
                            total = pade_weights[j] * image
                            if j:
                                total = osum[(side, comp, *place)] + total
                            osum[(side, comp, *place)] = total

                        surface(read, comp, r, pade_decays[j], write)

    peers = sum(jnp.where(there, 1, 0) for there in (has_up, has_dn, slab_up, slab_dn))
    pl.semaphore_wait(barrier, peers)

    for copy in (*edge_loads, *ghosts0):
        copy.wait()
    pack(flat0, pu1, pd1, near1)
    start(first_near)
    pack(flat0, pu1, pd1, rest1)
    start(first_rest)

    for copy in (*inner_loads, m_load, c_load):
        copy.wait()
    first_sweep(inner, 0, planes)
    for copy in (*ghosts1, *aux_loads):
        copy.wait()

    @pl.loop(0, 2 * TERMS * 2)
    def _(p):
        pua[p] = flata[line(p, last), :]
        pda[p] = flata[line(p, PAD), :]

    start(aux_rows)
    arrived(first_near)
    unpack(flat0, ru1, rd1, near1)
    first_sweep(outer, 0, 4, planes - 4)

    second_sweep_ends(outer)
    pack(flat1, pu2, pd2, near2)
    for p in range(6):
        pu2[6 + p] = flatt[line(p, last), :]
        pd2[6 + p] = flatt[line(p, PAD), :]
    start(second_near)

    arrived(first_rest)
    unpack(flat0, ru1, rd1, rest1)
    first_sweep(outer, 2, planes - 2)
    pack(flat1, pu2, pd2, rest2)
    start(second_rest)

    second_sweep_ends(inner)
    aux_surface(inner)
    arrived(aux_rows)
    for there, source, row in ((has_dn, rua, PAD - 1), (has_up, rda, last + 1)):

        @pl.when(there)
        def _():
            @pl.loop(0, 2 * TERMS * 2)
            def _(p):
                flata[line(p, row), :] = source[p]

    aux_surface(outer)

    arrived(second_near)
    unpack(flat1, ru2, rd2, near2)

    @pl.when(has_dn)
    def _():
        for side, (x, z, z_below) in enumerate(((0, 1, None), (4, 5, 3))):
            g = ru2[10 + side]
            row = pd2[x]
            slope = row - row_behind(row) + pd2[z]
            if z_below is not None:
                slope = slope - pd2[z_below]
            flatt[line(2 * side, PAD - 1), :] = ru2[6 + 2 * side] + g * row
            flatt[line(2 * side + 1, PAD - 1), :] = ru2[7 + 2 * side] - g * slope

    @pl.when(has_up)
    def _():
        for side, x in enumerate((0, 4)):
            g = rd2[10 + side]
            flatt[line(2 * side, last + 1), :] = rd2[6 + 2 * side] + g * pu2[x]
            flatt[line(2 * side + 1, last + 1), :] = rd2[7 + 2 * side]

    second_sweep_ends(outer)
    weight = sum(pade_weights)

    @pl.loop(0, 2)
    def _(side):
        for comp in range(2):
            for r in range(tiles):

                def read(c, row):
                    return tr[side * 2 + comp, c, pl.ds(row, 8), :]

                def write(c, u, image):
                    place = (side, comp, pl.ds(8 * r, 8), pl.ds(c * LANES, LANES))
                    out[place] = (u + weight * image) - osum[place]
                    osum[place] = image

                surface(read, comp, r, 1.0, write)

    @pl.when(slab_up)
    def _():
        slab_goes_up.start()

    @pl.when(slab_dn)
    def _():
        slab_goes_dn.start()

    second_sweep_inner(inner)

    @pl.loop(0, 2)
    def _(side):
        for comp in range(2):
            for r in range(tiles):
                for c in range(cols):
                    place = (pl.ds(8 * r, 8), pl.ds(c * LANES, LANES))
                    image = osum[(side, comp, *place)]
                    for j in range(TERMS):
                        where = (0, side, j, comp, *place)
                        next_aux[where] = image - next_aux[where]

    arrived(second_rest)
    unpack(flat1, ru2, rd2, rest2)
    second_sweep_inner(outer)

    for pair in (first_near, first_rest, aux_rows, second_near, second_rest):
        sent(pair)

    @pl.when(slab_dn)
    def _():
        slab_goes_up.wait_recv()
        slab_goes_dn.wait_send()

    @pl.when(slab_up)
    def _():
        slab_goes_dn.wait_recv()
        slab_goes_up.wait_send()


def store_kernel(field, face, aux, field_out, face_out, aux_out, sem):
    copies = [
        pltpu.make_async_copy(field.at[comp, pl.ds(k, half)], field_out.at[comp, pl.ds(k, half)], sem.at[i])
        for half in (field.shape[1] // 2,)
        for i, (comp, k) in enumerate((comp, k) for comp in range(3) for k in (0, half))
    ]
    copies += [
        pltpu.make_async_copy(aux.at[0, side, pl.ds(j, 2)], aux_out.at[0, side, pl.ds(j, 2)], sem.at[6 + 2 * side + j // 2])
        for side in range(2)
        for j in (0, 2)
    ]
    copies.append(pltpu.make_async_copy(face, face_out, sem.at[10]))
    for copy in copies:
        copy.start()
    for copy in copies:
        copy.wait()


def solution(mesh):
    n_slab, n_tile = mesh.shape["slab"], mesh.shape["tile"]

    def step(electric, current, mass_shift, interface, auxiliary):
        _, planes, rows, width = electric.shape
        cols = width // LANES
        tall = rows + 2 * PAD
        f32 = jnp.float32
        hbm = pl.BlockSpec(memory_space=pltpu.MemorySpace.HBM)
        vmem = pl.BlockSpec(memory_space=pltpu.VMEM)
        shapes = (electric.shape, interface.shape, auxiliary.shape)

        def lines(n):
            return pltpu.VMEM((n, cols, LANES), f32)

        held = pl.pallas_call(
            functools.partial(kernel, n_slab, n_tile),
            out_shape=tuple(pltpu.VMEM(shape, f32) for shape in shapes),
            in_specs=[hbm] * 5,
            out_specs=(vmem, vmem, vmem),
            scratch_shapes=[
                pltpu.VMEM((3, planes + 2, cols, tall, LANES), f32),
                pltpu.VMEM((3, planes + 2, cols, tall, LANES), f32),
                pltpu.VMEM(electric.shape, f32),
                pltpu.VMEM(mass_shift.shape, f32),
                pltpu.VMEM((2, TERMS, 2, cols, tall, LANES), f32),
                pltpu.VMEM((6, cols, tall, LANES), f32),
                pltpu.VMEM((2, 2, rows, width), f32),
                pltpu.VMEM((2, 2, rows, width), f32),
                *[lines(2 * planes)] * 4,
                *[lines(4 * TERMS)] * 4,
                *[lines(2 * planes + 6)] * 4,
                pltpu.SemaphoreType.DMA((9, cols)),
                pltpu.SemaphoreType.DMA((6, 2)),
                pltpu.SemaphoreType.DMA((6, 2)),
            ],
            compiler_params=pltpu.CompilerParams(
                collective_id=0, has_side_effects=True, vmem_limit_bytes=VMEM_LIMIT
            ),
        )(electric, current, mass_shift, interface, auxiliary)
        return pl.pallas_call(
            store_kernel,
            out_shape=tuple(jax.ShapeDtypeStruct(shape, f32) for shape in shapes),
            in_specs=[vmem] * 3,
            out_specs=(hbm, hbm, hbm),
            scratch_shapes=[pltpu.SemaphoreType.DMA((11,))],
            compiler_params=pltpu.CompilerParams(vmem_limit_bytes=2**20),
        )(*held)

    placed = (
        P(None, "slab", "tile", None),
        P(None, "slab", "tile", None),
        P("slab", "tile", None),
        P("slab", None, None, "tile", None),
        P("slab", None, None, None, "tile", None),
    )
    return jax.shard_map(
        step,
        mesh=mesh,
        in_specs=placed,
        out_specs=(
            P(None, "slab", "tile", None),
            P("slab", None, None, "tile", None),
            P("slab", None, None, None, "tile", None),
        ),
        check_vma=False,
    )
```

time: 40.6 us -> 29.2 us (0.72)
  Pallas kernels: 34.2 us -> 28.4 us
  local copies, waits for them, and re-layouts: 5.59 us -> 0 us
    pallas_call x1 -> x2, Pallas kernels: 34.2 us -> 28.4 us  [the longest x1 25.1 us: step(): pl.pallas_call(functools.partial(kernel, n_slab, n_tile), out_shape=tuple...]
    unnamed x5 -> x0, local copies, waits for them, and re-layouts: 5.59 us -> none
where the time goes in v2:
time: 29.2 us; the launch traced here: 29 us
  Pallas kernels  28.4 us (97%)
  between operations  0.64 us (2%)
    pallas_call x1, Pallas kernels, step(): pl.pallas_call(functools.partial(kernel, n_slab, n_tile), out_shape=tuple...  25.1 us
    pallas_call x1, Pallas kernels, step(): pl.pallas_call(store_kernel, out_shape=tuple((jax.ShapeDtypeStruct(shape,...  3.31 us

profile of v2, /device:TPU:97, one launch (start us, length us, event | category | flops | bytes accessed | tf_op | source)
XLA Modules:
  0.0 29.0 jit_solution(5008195832113631216)
XLA Ops:
  0.6 25.1 %shard_map.76 = (f32[3,14,32,1024]{3,2,1,0:T(8,128)S(1)}, f32[1,2,2,32,1024]{4,3,2,1,0:T(8,128)S(1)}, f32[1,2,4,2,32,1024]{5,4,3,2,1,0:T(8,128)S(1)}) custom-call(f32[3,14,32,1024]{3,2,1,0:T(8,128)} %electric.1, f32[3,14,32,1024]{3,2,1,0:T(8,128)} %current.1, f32[14,32,1024]{2,1,0:T(8,128)} %mass.1, f32[1,2,2,32,1024]{4,3,2,1,0:T(8,128)} %interface.1, ...), custom_call_target="tpu_custom_call" | custom-call | tf_op jit(solution)/shard_map/pallas_call | solution.py:587
  25.7 3.3 %shard_map.77 = (f32[3,14,32,1024]{3,2,1,0:T(8,128)}, f32[1,2,2,32,1024]{4,3,2,1,0:T(8,128)}, f32[1,2,4,2,32,1024]{5,4,3,2,1,0:T(8,128)}) custom-call(f32[3,14,32,1024]{3,2,1,0:T(8,128)S(1)} %get-tuple-element.6.field, f32[1,2,2,32,1024]{4,3,2,1,0:T(8,128)S(1)} %get-tuple-element.7.face, f32[1,2,4,2,32,1024]{5,4,3,2,1,0:T(8,128)S(1)} %get-tuple-element.8.aux), custom_call_target="tpu_custom_call" | custom-call | tf_op jit(solution)/shard_map/pallas_call | solution.py:612
